TPU v7x, 8 devices: a whole 2x2x1 slice. The times are simulated.
8 devices in a mesh: dp: 1 (over z), cx: 2 (over y), cy: 4 (over x, core).
Axes of the slice: x: 2, y: 2, z: 1, core: 2. Of those that a mesh axis runs over, the one named last changes fastest.
Arguments:
- x: bfloat16 [1, 2048, 1536], P('dp', ('cx', 'cy'))
- w_qkv: bfloat16 [1536, 4608], replicated
- w_o: bfloat16 [24, 64, 1536], replicated
Outputs:
- output: bfloat16 [1, 2048, 1536], P('dp', ('cx', 'cy'))
All inputs are finite; a program needn't handle non-finite values.
Results may differ from a plain program's by a relative error of at most 0.00800223.
Values are sent between devices in bfloat16 or wider.
A program may use at most 1 GiB of HBM per device.

v0:
```python
import jax
import jax.numpy as jnp
from jax import lax
from jax.sharding import PartitionSpec as P


def solution(mesh):
    def attend_local(x_blk, w_qkv, w_o):
        num_heads, head_dim = w_o.shape[0], w_o.shape[1]
        tok_rows = x_blk.shape[1]
        inv_sqrt = head_dim ** -0.5
        qkv_rows = jnp.dot(x_blk[0], w_qkv, preferred_element_type=jnp.float32).astype(jnp.bfloat16)
        qkv_rows = lax.all_to_all(qkv_rows.reshape(tok_rows, 3, num_heads, head_dim), "cy", 2, 0, tiled=True)
        kv_all = lax.all_gather(qkv_rows[:, 1:], "cx", axis=0, tiled=True)
        logits = jnp.einsum("qhd,khd->hqk", qkv_rows[:, 0], kv_all[:, 0], preferred_element_type=jnp.float32) * inv_sqrt
        row_max = jnp.max(logits, axis=-1, keepdims=True)
        weights = jnp.exp(logits - row_max)
        row_sum = jnp.sum(weights, axis=-1, keepdims=True)
        attn_rows = jnp.einsum("hqk,khd->qhd", weights.astype(jnp.bfloat16), kv_all[:, 1], preferred_element_type=jnp.float32)
        attn_rows = (attn_rows / jnp.transpose(row_sum, (1, 0, 2))).astype(jnp.bfloat16)
        attn_rows = lax.all_to_all(attn_rows, "cy", 0, 1, tiled=True)
        result = jnp.einsum("thd,hdc->tc", attn_rows, w_o, preferred_element_type=jnp.float32)
        return result.astype(jnp.bfloat16)[None]

    return jax.shard_map(attend_local, mesh=mesh, in_specs=(P("dp", ("cx", "cy"), None), P(None, None), P(None, None, None)), out_specs=P("dp", ("cx", "cy"), None), check_vma=False)
```

profile of v0, /device:TPU:0, one launch (start us, length us, event | category | flops | bytes accessed | tf_op | source)
XLA Modules:
  0.0 198.4 jit_solution(16959461928684504787)
XLA Ops:
  6.5 0.0 copy-start
  6.5 0.0 all-gather.2.cloned.1.call-start
  6.5 1.1 copy-done
  7.7 10.1 %convolution_convert_fusion = bf16[256,4608]{1,0:T(8,128)(2,1)} fusion(bf16[1536,4608]{1,0:T(8,128)(2,1)} %param.4, bf16[1,256,1536]{2,1,0:T(8,128)(2,1)S(1)} %copy-done), kind=kOutput, calls=%fused_computation.5 | convolution fusion | flops 3625058304 | bytes 17301504 | tf_op jit(solution)/shard_map/dot_general | solution.py:12
  17.8 2.8 %copy.9 = bf16[256,4608]{0,1:T(8,128)(2,1)S(1)} copy(bf16[256,4608]{1,0:T(8,128)(2,1)} %convolution_convert_fusion) | data formatting | bytes 4718592 | tf_op jit(solution)/shard_map/convert_element_type | solution.py:12
  20.6 0.3 copy.10
  20.9 32.9 %all_to_all.36 = bf16[256,3,24,64]{0,3,1,2:T(8,128)(2,1)S(1)} all-to-all(bf16[256,3,24,64]{0,3,1,2:T(8,128)(2,1)S(1)} %copy.10), channel_id=1, replica_groups=mesh['dp'=1,'cx'=2,'cy'=4] {'cy'}, dimensions={2} | all-to-all | bytes 4718592 | tf_op jit(solution)/shard_map/all_to_all | solution.py:13
  53.8 2.0 %copy.12 = bf16[4,256,3,6,64]{1,0,4,3,2:T(4,128)(2,1)S(1)} copy(bf16[4,256,3,6,64]{1,4,2,3,0:T(8,128)(2,1)S(1)} %bitcast.49) | data formatting | bytes 4718592 | tf_op jit(solution)/shard_map/all_to_all | solution.py:13
  55.9 2.9 %all_to_all.29 = bf16[1024,3,6,64]{0,3,2,1:T(8,128)(2,1)} reshape(bf16[4,256,3,6,64]{1,0,4,3,2:T(4,128)(2,1)S(1)} %copy.12) | data formatting | bytes 4718592 | tf_op jit(solution)/shard_map/all_to_all | solution.py:13
  58.8 2.7 %slice.16 = bf16[1024,2,6,64]{0,3,2,1:T(8,128)(2,1)} slice(bf16[1024,3,6,64]{0,3,2,1:T(8,128)(2,1)} %all_to_all.29), slice={[0:1024], [1:3], [0:6], [0:64]} | slice | bytes 3145728 | tf_op jit(solution)/shard_map/slice | solution.py:14
  61.5 0.0 all-gather.2.cloned.1.call-update
  61.5 42.4 %all-gather.2.cloned.1.call-done = bf16[2048,2,6,64]{0,3,2,1:T(8,128)(2,1)} async-done(((bf16[1024,2,6,64]{0,3,2,1:T(8,128)(2,1)}), bf16[2048,2,6,64]{0,3,2,1:T(8,128)(2,1)}) %all-gather.2.cloned.1.call-update) | async-done | bytes 3145744 | tf_op jit(solution)/shard_map/all_gather | solution.py:14
  103.9 21.0 %multiply_reduce_fusion = (f32[6,1024]{1,0:T(8,128)S(1)}, f32[6,1024,2048]{2,1,0:T(8,128)}) fusion(bf16[2048,2,6,64]{0,3,2,1:T(8,128)(2,1)} %all-gather.2.cloned.1.call-done, bf16[1024,3,6,64]{0,3,2,1:T(8,128)(2,1)} %all_to_all.29), kind=kOutput, calls=%fused_computation.1 | convolution fusion | flops 1635772416 | bytes 52715520 | tf_op jit(solution)/shard_map/qhd,khd->hqk/dot_general | solution.py:15
  124.9 0.0 copy-start.2
  124.9 20.6 %fusion = f32[6,1024]{1,0:T(8,128)S(1)} fusion(f32[6,1024,2048]{2,1,0:T(8,128)} %get-tuple-element.6, f32[6,1024]{1,0:T(8,128)S(1)} %get-tuple-element.5), kind=kLoop, calls=%fused_computation.2 | loop fusion | flops 37742592 | bytes 50380800 | tf_op jit(solution)/shard_map/reduce_sum | solution.py:18
  145.5 0.0 copy-done.2
  145.5 18.6 %fusion.7 = bf16[1024,6,64]{0,2,1:T(8,128)(2,1)S(1)} fusion(f32[6,1024,2048]{2,1,0:T(8,128)} %get-tuple-element.6, f32[6,1024]{1,0:T(8,128)S(1)} %get-tuple-element.5, bf16[2048,2,6,64]{0,3,2,1:T(8,128)(2,1)S(1)} %copy-done.2, f32[1024,6]{0,1:T(8,128)S(1)} %bitcast.51), kind=kOutput, calls=%fused_computation.13 | convolution fusion | flops 1649147904 | bytes 52756480 | tf_op jit(solution)/shard_map/hqk,khd->qhd/dot_general | solution.py:19
  164.1 1.7 copy.13
  165.8 1.5 reshape.6
  167.3 14.6 %all_to_all.37 = bf16[4,2,49152]{2,1,0:T(2,128)(2,1)} all-to-all(bf16[4,2,49152]{2,1,0:T(2,128)(2,1)S(1)} %reshape.6), channel_id=1, replica_groups=mesh['dp'=1,'cx'=2,'cy'=4] {'cy'}, dimensions={0} | all-to-all | bytes 1572864 | tf_op jit(solution)/shard_map/all_to_all | solution.py:21
  182.0 2.9 %reshape.7 = bf16[1024,6,64]{2,1,0:T(8,128)(2,1)S(1)} reshape(bf16[4,2,49152]{2,1,0:T(2,128)(2,1)} %all_to_all.37) | data formatting | bytes 1572864
  184.9 1.7 copy.14
  186.6 0.0 copy-start.1
  186.6 4.9 %fusion.5 = bf16[1,256,1536]{2,1,0:T(8,128)(2,1)} fusion(bf16[256,24,64]{0,2,1:T(8,128)(2,1)} %bitcast.52, bf16[24,64,1536]{2,1,0:T(8,128)(2,1)} %param.5), kind=kOutput, calls=%fused_computation.8 | convolution fusion | flops 1208352768 | bytes 6291456 | tf_op jit(solution)/shard_map/thd,hdc->tc/dot_general | solution.py:22
  191.5 0.0 copy-done.1
Async XLA Ops:
  6.5 1.1 copy-start
  6.5 97.4 %all-gather.2.cloned.1.call-start = ((), (), s32[]{:S(2)}) async-start(), calls=%async_computation.2 | async-start | bytes 4718592 | tf_op jit(solution)/shard_map/all_gather | solution.py:14
  124.9 20.6 %copy-start.2 = (bf16[2048,2,6,64]{0,3,2,1:T(8,128)(2,1)S(1)}, bf16[2048,2,6,64]{0,3,2,1:T(8,128)(2,1)}, u32[]{:S(2)}) copy-start(bf16[2048,2,6,64]{0,3,2,1:T(8,128)(2,1)} %all-gather.2.cloned.1.call-done) | copy-start | bytes 9437188
  186.6 4.9 %copy-start.1 = (bf16[1,256,1536]{2,1,0:T(8,128)(2,1)S(1)}, bf16[1,256,1536]{2,1,0:T(8,128)(2,1)}, u32[]{:S(2)}) copy-start(bf16[1,256,1536]{2,1,0:T(8,128)(2,1)} %param.3) | copy-start | bytes 2359300
Sparse Core Ops, SparseCore 0:
  61.6 42.2 all-gather.1
where the time goes:
time: 199 us; the launch traced here: 198 us
  matrix products  54.7 us (27%)
  blocking collectives  47.5 us (24%)
  waiting for transfers between devices  42.4 us (21%)
  other arithmetic  20.6 us (10%)
  local copies, waits for them, and re-layouts  19.7 us (10%)
  between operations  13.5 us (7%)
    all_gather x1, waiting for transfers between devices, attend_local(): kv_all = lax.all_gather(qkv_rows[:, 1:], 'cx', axis=0, tiled=True)  42.4 us
    all_to_all x1, blocking collectives, attend_local(): lax.all_to_all(qkv_rows.reshape(tok_rows, 3, num_heads, head_dim), 'cy',...  32.9 us
    dot_general x1, matrix products, attend_local(): jnp.einsum('qhd,khd->hqk', qkv_rows[:, 0], kv_all[:, 0], preferred_elemen...  21 us
    reduce_sum x1, other arithmetic, attend_local(): row_sum = jnp.sum(weights, axis=-1, keepdims=True)  20.6 us
    dot_general x1, matrix products, attend_local(): jnp.einsum('hqk,khd->qhd', weights.astype(jnp.bfloat16), kv_all[:, 1], pr...  18.6 us
    all_to_all x1, blocking collectives, attend_local(): attn_rows = lax.all_to_all(attn_rows, 'cy', 0, 1, tiled=True)  14.6 us
    dot_general x1, matrix products, attend_local(): jnp.dot(x_blk[0], w_qkv, preferred_element_type=jnp.float32)  10.1 us
    unnamed x8, local copies, waits for them, and re-layouts  5.54 us
  transfers between devices with their start and end apart: 1, of which 1 were waited for; matrix products, arithmetic and copies ran while one was open for 0% of the time, Pallas kernels for 0%

commit v1 on v0

v1 whole, which is shorter than its diff:
```python
import math

import jax
import jax.numpy as jnp
from jax import lax
from jax.experimental import pallas as pl
from jax.experimental.pallas import tpu as pltpu
from jax.sharding import PartitionSpec as P

MESH = pl.DeviceIdType.MESH
BF16 = jnp.bfloat16
F32 = jnp.float32
NSUB = 2


def _nt(a, b):
    return lax.dot_general(a, b, (((1,), (1,)), ((), ())), preferred_element_type=F32)


def _tn(a, b):
    return lax.dot_general(a, b, (((0,), (0,)), ((), ())), preferred_element_type=F32)


def _nn(a, b):
    return lax.dot_general(a, b, (((1,), (0,)), ((), ())), preferred_element_type=F32)


def _kernel(dims, x_hbm, wqkv_hbm, wo_hbm, y_ref,
            xs, wq, wk, wv, wvt, wo, ks, vts, qz, ms, ls, acc, osend, omine, orecv,
            wsem, ssem, rsem, osem):
    tok, width, heads, hd = dims
    cols = heads * hd
    half = tok // 2
    sub = half // NSUB
    scale = (hd ** -0.5) * math.log2(math.e)

    dp, cx, cy = lax.axis_index("dp"), lax.axis_index("cx"), lax.axis_index("cy")
    core = lax.rem(cy, 2)
    mate = (dp, cx, cy + 1 - 2 * core)
    xn = (dp, cx, lax.rem(cy + 2, 4))
    yn = (dp, 1 - cx, cy)

    def wcopy(i, src, dst):
        return pltpu.make_async_copy(src, dst, wsem.at[i])

    g0 = pl.multiple_of(core * cols, cols)
    g1 = pl.multiple_of((1 - core) * cols, cols)
    loads = [
        wcopy(0, x_hbm, xs.at[0, pl.ds(0, tok), :]),
        wcopy(1, wqkv_hbm.at[:, pl.ds(g0, cols)], wq),
        wcopy(2, wqkv_hbm.at[:, pl.ds(pl.multiple_of(g0 + width, cols), cols)], wk),
        wcopy(3, wqkv_hbm.at[:, pl.ds(pl.multiple_of(g0 + 2 * width, cols), cols)], wv),
        wcopy(4, wo_hbm.at[pl.ds(g0, cols), :], wo.at[0]),
        wcopy(5, wo_hbm.at[pl.ds(g1, cols), :], wo.at[1]),
    ]
    for ld in loads:
        ld.start()

    barrier = pltpu.get_barrier_semaphore()
    for other in (mate, xn, yn):
        pl.semaphore_signal(barrier, inc=1, device_id=other, device_id_type=MESH)
    pl.semaphore_wait(barrier, 3)

    started = []

    def send(i, stage_from, row_from, stage_to, row_to, rows, dev):
        c = pltpu.make_async_remote_copy(
            src_ref=xs.at[stage_from, pl.ds(row_from, rows), :],
            dst_ref=xs.at[stage_to, pl.ds(row_to, rows), :],
            send_sem=ssem.at[i], recv_sem=rsem.at[i],
            device_id=dev, device_id_type=MESH)
        return c

    copies = {}
    n = 0

    def define(key, *a):
        nonlocal n
        copies[key] = send(n, *a)
        n += 1

    define(("own",), 0, 0, 0, tok, tok, mate)
    for st, hx, hy in ((1, 1, 0), (2, 0, 1)):
        for u in range(NSUB):
            define(("x", st, u), 0, hx * half + u * sub, st, u * sub, sub, xn)
            define(("y", st, u), 0, hy * half + u * sub, st, half + u * sub, sub, yn)
            define(("fx", st, u), st, u * sub, st, tok + u * sub, sub, mate)
            define(("fy", st, u), st, half + u * sub, st, tok + half + u * sub, sub, mate)
    for u in range(NSUB):
        define(("x", 3, u), 1, half + u * sub, 3, u * sub, sub, xn)
        define(("y", 3, u), 1, u * sub, 3, half + u * sub, sub, yn)
        define(("fx", 3, u), 3, u * sub, 3, tok + u * sub, sub, mate)
        define(("fy", 3, u), 3, half + u * sub, 3, tok + half + u * sub, sub, mate)

    def start(key):
        copies[key].start()
        started.append(key)

    loads[0].wait()
    start(("own",))
    for st in (1, 2):
        for u in range(NSUB):
            start(("x", st, u))
            start(("y", st, u))

    def project(st, r0):
        rows = xs[st, pl.ds(r0, tok), :]
        ks[pl.ds(r0, tok), :] = _nn(rows, wk[...]).astype(BF16)
        vts[:, pl.ds(r0, tok)] = _nt(wvt[...], rows).astype(BF16)

    def project_q(r0):
        rows = xs[0, pl.ds(r0, tok), :]
        qt = _nn(rows, wq[...]).T.astype(BF16)
        for h in range(heads):
            e = (h % 2) * hd
            qz[h, pl.ds(e, hd), pl.ds(r0, tok)] = qt[h * hd:(h + 1) * hd, :]

    def attend(st):
        def pair(j, carry):
            kp = ks[:, pl.ds(pl.multiple_of(j * 2 * hd, 2 * hd), 2 * hd)]
            for e in range(2):
                h = 2 * j + e
                s = _nn(kp, qz[h])
                mc = jnp.max(s, axis=0, keepdims=True)
                vt = vts[pl.ds(pl.multiple_of(h * hd, hd), hd), :]
                if st == 0:
                    m = mc
                else:
                    m = jnp.maximum(ms[h], mc)
                    alpha = jnp.exp2((ms[h] - m) * scale)
                p = jnp.exp2((s - m) * scale)
                lc = jnp.sum(p, axis=0, keepdims=True)
                o = _nn(vt, p.astype(BF16))
                if st == 0:
                    ls[h] = lc
                    acc[h] = o
                else:
                    ls[h] = ls[h] * alpha + lc
                    acc[h] = acc[h] * alpha + o
                ms[h] = m
            return carry

        lax.fori_loop(0, heads // 2, pair, 0)

    for h in range(heads):
        e = ((h + 1) % 2) * hd
        qz[h, pl.ds(e, hd), :] = jnp.zeros((hd, 2 * tok), BF16)
    loads[1].wait()
    project_q(0)
    loads[2].wait()
    loads[3].wait()
    wvt[...] = wv[...].T
    project(0, 0)
    copies[("own",)].wait_recv()
    project_q(tok)
    project(0, tok)
    attend(0)
    for st in (1, 2, 3):
        for u in range(NSUB):
            copies[("x", st, u)].wait_recv()
            start(("fx", st, u))
            if st == 1:
                start(("y", 3, u))
            copies[("y", st, u)].wait_recv()
            start(("fy", st, u))
            if st == 1:
                start(("x", 3, u))
        project(st, 0)
        for u in range(NSUB):
            copies[("fx", st, u)].wait_recv()
            copies[("fy", st, u)].wait_recv()
        project(st, tok)
        attend(st)

    for h in range(heads):
        o = (acc[h] / ls[h]).T.astype(BF16)
        omine[:, pl.ds(h * hd, hd)] = o[:tok]
        osend[:, pl.ds(h * hd, hd)] = o[tok:]
    oc = pltpu.make_async_remote_copy(
        src_ref=osend, dst_ref=orecv, send_sem=osem.at[0], recv_sem=osem.at[1],
        device_id=mate, device_id_type=MESH)
    oc.start()
    loads[4].wait()
    loads[5].wait()
    y = _nn(omine[...], wo[0])
    oc.wait_recv()
    y_ref[...] = (y + _nn(orecv[...], wo[1])).astype(BF16)
    oc.wait_send()
    for key in started:
        copies[key].wait_send()


def solution(mesh):
    def body(x, w_qkv, w_o):
        tok, width = x.shape[1], x.shape[2]
        heads_all, hd = w_o.shape[0], w_o.shape[1]
        heads = heads_all // 2
        cols = heads * hd
        ncopy = 1 + 3 * 4 * NSUB
        y = pl.pallas_call(
            lambda *r: _kernel((tok, width, heads, hd), *r),
            out_shape=jax.ShapeDtypeStruct((tok, width), BF16),
            in_specs=[pl.BlockSpec(memory_space=pl.ANY)] * 3,
            out_specs=pl.BlockSpec(memory_space=pltpu.VMEM),
            scratch_shapes=[
                pltpu.VMEM((4, 2 * tok, width), BF16),
                pltpu.VMEM((width, cols), BF16),
                pltpu.VMEM((width, cols), BF16),
                pltpu.VMEM((width, cols), BF16),
                pltpu.VMEM((cols, width), BF16),
                pltpu.VMEM((2, cols, width), BF16),
                pltpu.VMEM((2 * tok, cols), BF16),
                pltpu.VMEM((cols, 2 * tok), BF16),
                pltpu.VMEM((heads, 2 * hd, 2 * tok), BF16),
                pltpu.VMEM((heads, 1, 2 * tok), F32),
                pltpu.VMEM((heads, 1, 2 * tok), F32),
                pltpu.VMEM((heads, hd, 2 * tok), F32),
                pltpu.VMEM((tok, cols), BF16),
                pltpu.VMEM((tok, cols), BF16),
                pltpu.VMEM((tok, cols), BF16),
                pltpu.SemaphoreType.DMA((6,)),
                pltpu.SemaphoreType.DMA((ncopy,)),
                pltpu.SemaphoreType.DMA((ncopy,)),
                pltpu.SemaphoreType.DMA((2,)),
            ],
            compiler_params=pltpu.CompilerParams(
                collective_id=0, has_side_effects=True, vmem_limit_bytes=60 * 1024 * 1024),
            name="dit_attention",
        )(x[0], w_qkv, w_o.reshape(heads_all * hd, width))
        return y[None]

    return jax.shard_map(
        body, mesh=mesh,
        in_specs=(P("dp", ("cx", "cy"), None), P(None, None), P(None, None, None)),
        out_specs=P("dp", ("cx", "cy"), None), check_vma=False)
```

time: 199 us -> 54.1 us (0.27)
  matrix products: 54.7 us -> 0 us
  Pallas kernels: 0 us -> 51.9 us
  blocking collectives: 47.5 us -> 0 us
  waiting for transfers between devices: 42.4 us -> 0 us
  other arithmetic: 20.6 us -> 0 us
  local copies, waits for them, and re-layouts: 19.7 us -> 2.06 us
  between operations: 13.5 us -> 0.01 us
    dot_general x4 -> x0, matrix products: 54.7 us -> none  [the longest x1 21 us: attend_local(): jnp.einsum('qhd,khd->hqk', qkv_rows[:, 0], kv_all[:, 0], preferred_elemen...]
    pallas_call x0 -> x1, Pallas kernels: none -> 51.9 us  [body(): pl.pallas_call(lambda *r: _kernel((tok, width, heads, hd), *r), out_shape...]
    all_to_all x2 -> x0, blocking collectives: 47.5 us -> none  [the longest x1 32.9 us: attend_local(): lax.all_to_all(qkv_rows.reshape(tok_rows, 3, num_heads, head_dim), 'cy',...]
    all_gather x1 -> x0, waiting for transfers between devices: 42.4 us -> none  [attend_local(): kv_all = lax.all_gather(qkv_rows[:, 1:], 'cx', axis=0, tiled=True)]
    reduce_sum x1 -> x0, other arithmetic: 20.6 us -> none  [attend_local(): row_sum = jnp.sum(weights, axis=-1, keepdims=True)]
    all_to_all x3 -> x0, local copies, waits for them, and re-layouts: 6.73 us -> none  [the longest x2 4.99 us: attend_local(): lax.all_to_all(qkv_rows.reshape(tok_rows, 3, num_heads, head_dim), 'cy',...]
    convert_element_type x2 -> x0, local copies, waits for them, and re-layouts: 4.49 us -> none  [the longest x1 2.83 us: attend_local(): jnp.dot(x_blk[0], w_qkv, preferred_element_type=jnp.float32)]
    unnamed x8 -> x1, local copies, waits for them, and re-layouts: 5.54 us -> 2.06 us
  transfers between devices with their start and end apart: 1 -> 0, of which waited for: 1 -> 0; matrix products, arithmetic and copies ran while one was open for 0% -> 0% of each run, Pallas kernels for 0% -> 0%
where the time goes in v1:
time: 54.1 us; the launch traced here: 54 us
  Pallas kernels  51.9 us (96%)
  local copies, waits for them, and re-layouts  2.06 us (4%)
    pallas_call x1, Pallas kernels, body(): pl.pallas_call(lambda *r: _kernel((tok, width, heads, hd), *r), out_shape...  51.9 us
    unnamed x1, local copies, waits for them, and re-layouts  2.06 us

profile of v1, /device:TPU:0, one launch (start us, length us, event | category | flops | bytes accessed | tf_op | source)
XLA Modules:
  0.0 54.0 jit_solution(544569450535394505)
XLA Ops:
  0.0 51.9 %dit_attention.1 = bf16[256,1536]{1,0:T(8,128)(2,1)} custom-call(bf16[256,1536]{1,0:T(8,128)(2,1)} %bitcast.5, bf16[1536,4608]{1,0:T(8,128)(2,1)} %r_1_.1, bf16[1536,1536]{1,0:T(8,128)(2,1)} %bitcast.3), custom_call_target="tpu_custom_call" | custom-call | tf_op jit(solution)/shard_map/dit_attention/pallas_call | solution.py:200
  51.9 2.1 %copy.5 = bf16[1,256,1536]{2,1,0:T(8,128)(2,1)} copy(bf16[1,256,1536]{2,1,0:T(8,128)(2,1)} %bitcast.4) | data formatting | bytes 1572864

commit v2 on v1

--- a/solution.py
+++ b/solution.py
@@ -27,6 +27,7 @@
 
 def _kernel(dims, x_hbm, wqkv_hbm, wo_hbm, y_ref,
             xs, wq, wk, wv, wvt, wo, ks, vts, qz, ms, ls, acc, osend, omine, orecv,
+            sb0, sb1, mb0, mb1,
             wsem, ssem, rsem, osem):
     tok, width, heads, hd = dims
     cols = heads * hd
@@ -115,29 +116,46 @@
             e = (h % 2) * hd
             qz[h, pl.ds(e, hd), pl.ds(r0, tok)] = qt[h * hd:(h + 1) * hd, :]
 
-    def attend(st):
+    def scores(h, pair, rows, r0, sb, mb):
+        kp = ks[pl.ds(r0, rows), pl.ds(pl.multiple_of(pair * 2 * hd, 2 * hd), 2 * hd)]
+        s = _nn(kp, qz[h])
+        sb[pl.ds(0, rows), :] = s
+        mb[...] = jnp.max(s, axis=0, keepdims=True)
+
+    def fold(h, rows, r0, sb, mb, first):
+        m = mb[...]
+        if not first:
+            m = jnp.maximum(ms[h], m)
+            alpha = jnp.exp2((ms[h] - m) * scale)
+        p = jnp.exp2((sb[pl.ds(0, rows), :] - m) * scale)
+        l = jnp.sum(p, axis=0, keepdims=True)
+        o = _nn(vts[pl.ds(pl.multiple_of(h * hd, hd), hd), pl.ds(r0, rows)], p.astype(BF16))
+        if not first:
+            l = ls[h] * alpha + l
+            o = acc[h] * alpha + o
+        return m, l, o
+
+    def keep(h, mlo):
+        ms[h], ls[h], acc[h] = mlo
+
+    def attend(rows, r0, first=False, last=False):
+        scores(0, 0, rows, r0, sb0, mb0)
+
         def pair(j, carry):
-            kp = ks[:, pl.ds(pl.multiple_of(j * 2 * hd, 2 * hd), 2 * hd)]
-            for e in range(2):
-                h = 2 * j + e
-                s = _nn(kp, qz[h])
-                mc = jnp.max(s, axis=0, keepdims=True)
-                vt = vts[pl.ds(pl.multiple_of(h * hd, hd), hd), :]
-                if st == 0:
-                    m = mc
-                else:
-                    m = jnp.maximum(ms[h], mc)
-                    alpha = jnp.exp2((ms[h] - m) * scale)
-                p = jnp.exp2((s - m) * scale)
-                lc = jnp.sum(p, axis=0, keepdims=True)
-                o = _nn(vt, p.astype(BF16))
-                if st == 0:
-                    ls[h] = lc
-                    acc[h] = o
-                else:
-                    ls[h] = ls[h] * alpha + lc
-                    acc[h] = acc[h] * alpha + o
-                ms[h] = m
+            nxt = jnp.minimum(j + 1, heads // 2 - 1)
+            scores(2 * j + 1, j, rows, r0, sb1, mb1)
+            even = fold(2 * j, rows, r0, sb0, mb0, first)
+            if not last:
+                keep(2 * j, even)
+            scores(2 * nxt, nxt, rows, r0, sb0, mb0)
+            odd = fold(2 * j + 1, rows, r0, sb1, mb1, first)
+            if not last:
+                keep(2 * j + 1, odd)
+            else:
+                o = jnp.concatenate([even[2] / even[1], odd[2] / odd[1]], axis=0).T.astype(BF16)
+                at = pl.ds(pl.multiple_of(j * 2 * hd, 2 * hd), 2 * hd)
+                omine[:, at] = o[:tok]
+                osend[:, at] = o[tok:]
             return carry
 
         lax.fori_loop(0, heads // 2, pair, 0)
@@ -154,7 +172,7 @@
     copies[("own",)].wait_recv()
     project_q(tok)
     project(0, tok)
-    attend(0)
+    attend(2 * tok, 0, first=True)
     for st in (1, 2, 3):
         for u in range(NSUB):
             copies[("x", st, u)].wait_recv()
@@ -170,12 +188,8 @@
             copies[("fx", st, u)].wait_recv()
             copies[("fy", st, u)].wait_recv()
         project(st, tok)
-        attend(st)
-
-    for h in range(heads):
-        o = (acc[h] / ls[h]).T.astype(BF16)
-        omine[:, pl.ds(h * hd, hd)] = o[:tok]
-        osend[:, pl.ds(h * hd, hd)] = o[tok:]
+        attend(2 * tok, 0, last=st == 3)
+
     oc = pltpu.make_async_remote_copy(
         src_ref=osend, dst_ref=orecv, send_sem=osem.at[0], recv_sem=osem.at[1],
         device_id=mate, device_id_type=MESH)
@@ -218,6 +232,10 @@
                 pltpu.VMEM((tok, cols), BF16),
                 pltpu.VMEM((tok, cols), BF16),
                 pltpu.VMEM((tok, cols), BF16),
+                pltpu.VMEM((2 * tok, 2 * tok), F32),
+                pltpu.VMEM((2 * tok, 2 * tok), F32),
+                pltpu.VMEM((1, 2 * tok), F32),
+                pltpu.VMEM((1, 2 * tok), F32),
                 pltpu.SemaphoreType.DMA((6,)),
                 pltpu.SemaphoreType.DMA((ncopy,)),
                 pltpu.SemaphoreType.DMA((ncopy,)),

time: 54.1 us -> 45.2 us (0.84)
  Pallas kernels: 51.9 us -> 43 us
    pallas_call x1, Pallas kernels: 51.9 us -> 43 us  [body(): pl.pallas_call(lambda *r: _kernel((tok, width, heads, hd), *r), out_shape...]
where the time goes in v2:
time: 45.2 us; the launch traced here: 45 us
  Pallas kernels  43 us (95%)
  local copies, waits for them, and re-layouts  2.06 us (5%)
    pallas_call x1, Pallas kernels, body(): pl.pallas_call(lambda *r: _kernel((tok, width, heads, hd), *r), out_shape...  43 us
    unnamed x1, local copies, waits for them, and re-layouts  2.06 us

profile of v2, /device:TPU:0, one launch (start us, length us, event | category | flops | bytes accessed | tf_op | source)
XLA Modules:
  0.0 45.0 jit_solution(17012159923823572650)
XLA Ops:
  0.0 43.0 %dit_attention.1 = bf16[256,1536]{1,0:T(8,128)(2,1)} custom-call(bf16[256,1536]{1,0:T(8,128)(2,1)} %bitcast.5, bf16[1536,4608]{1,0:T(8,128)(2,1)} %r_1_.1, bf16[1536,1536]{1,0:T(8,128)(2,1)} %bitcast.3), custom_call_target="tpu_custom_call" | custom-call | tf_op jit(solution)/shard_map/dit_attention/pallas_call | solution.py:214
  43.0 2.1 %copy.5 = bf16[1,256,1536]{2,1,0:T(8,128)(2,1)} copy(bf16[1,256,1536]{2,1,0:T(8,128)(2,1)} %bitcast.4) | data formatting | bytes 1572864

commit v3 on v2

v3 whole, which is shorter than its diff:
```python
import math

import jax
import jax.numpy as jnp
from jax import lax
from jax.experimental import pallas as pl
from jax.experimental.pallas import tpu as pltpu
from jax.sharding import PartitionSpec as P

MESH = pl.DeviceIdType.MESH
BF16 = jnp.bfloat16
F32 = jnp.float32
UNROLL = 6
AHEAD = 3


def _nt(a, b):
    return lax.dot_general(a, b, (((1,), (1,)), ((), ())), preferred_element_type=F32)


def _tn(a, b):
    return lax.dot_general(a, b, (((0,), (0,)), ((), ())), preferred_element_type=F32)


def _nn(a, b):
    return lax.dot_general(a, b, (((1,), (0,)), ((), ())), preferred_element_type=F32)


def _kernel(dims, x_hbm, wqkv_hbm, o_ref,
            xs, wq, wk, wv, wvt, ks, vts, qz, ms, ls, acc, osend,
            sb0, sb1, sb2, mb0, mb1, mb2,
            wsem, ssem, rsem, osem):
    tok, width, heads, hd = dims
    cols = heads * hd
    scale = (hd ** -0.5) * math.log2(math.e)

    dp, cx, cy = lax.axis_index("dp"), lax.axis_index("cx"), lax.axis_index("cy")
    core = lax.rem(cy, 2)
    mate = (dp, cx, cy + 1 - 2 * core)
    xn = (dp, cx, lax.rem(cy + 2, 4))
    yn = (dp, 1 - cx, cy)

    def wcopy(i, src, dst):
        return pltpu.make_async_copy(src, dst, wsem.at[i])

    g0 = pl.multiple_of(core * cols, cols)
    loads = [
        wcopy(0, x_hbm, xs.at[pl.ds(0, tok), :]),
        wcopy(1, wqkv_hbm.at[:, pl.ds(g0, cols)], wq),
        wcopy(2, wqkv_hbm.at[:, pl.ds(pl.multiple_of(g0 + width, cols), cols)], wk),
        wcopy(3, wqkv_hbm.at[:, pl.ds(pl.multiple_of(g0 + 2 * width, cols), cols)], wv),
    ]
    for ld in loads:
        ld.start()

    barrier = pltpu.get_barrier_semaphore()
    for other in (mate, xn, yn):
        pl.semaphore_signal(barrier, inc=1, device_id=other, device_id_type=MESH)
    pl.semaphore_wait(barrier, 3)

    def copy(sem, row_from, row_to, rows, dev):
        return pltpu.make_async_remote_copy(
            src_ref=xs.at[pl.ds(row_from, rows), :], dst_ref=xs.at[pl.ds(row_to, rows), :],
            send_sem=ssem.at[sem], recv_sem=rsem.at[sem], device_id=dev, device_id_type=MESH)

    part = tok // 4
    x_from = [2 * part, 3 * part, 0, part, 2 * tok + part, 3 * tok + part]
    y_from = [0, part, 2 * part, 3 * part, 2 * tok, 3 * tok]
    from_x = [copy(s, x_from[s], (2 + s) * tok, part, xn) for s in range(6)]
    from_y = [copy(6 + s, y_from[s], (2 + s) * tok + part, part, yn) for s in range(6)]
    from_mate = [copy(12 + s, (2 + s) * tok, (2 + s) * tok + 2 * part, 2 * part, mate) for s in range(6)]
    own = copy(18, 0, tok, tok, mate)

    loads[0].wait()
    own.start()
    for s in range(4):
        from_x[s].start()
        from_y[s].start()

    def arrived(s):
        from_x[s].wait_recv()
        from_y[s].wait_recv()
        from_mate[s].start()
        if s < 2:
            from_x[4 + s].start()
            from_y[4 + s].start()
        if s > 0:
            from_mate[s - 1].wait_recv()

    def project_k(row, r0, rows):
        ks[pl.ds(r0, rows), :] = _nn(xs[pl.ds(row, rows), :], wk[...]).astype(BF16)

    def project_v(row, r0, rows):
        vts[:, pl.ds(r0, rows)] = _nt(wvt[...], xs[pl.ds(row, rows), :]).astype(BF16)

    def project_q(r0):
        rows = xs[pl.ds(r0, tok), :]
        qt = _nn(rows, wq[...]).T.astype(BF16)
        for h in range(heads):
            e = (h % 2) * hd
            qz[h, pl.ds(e, hd), pl.ds(r0, tok)] = qt[h * hd:(h + 1) * hd, :]

    def scores(h, pair, rows, r0, sb, mb):
        kp = ks[pl.ds(r0, rows), pl.ds(pl.multiple_of(pair * 2 * hd, 2 * hd), 2 * hd)]
        s = _nn(kp, qz[h])
        for b in range(2 * tok // 128):
            sb[b, pl.ds(0, rows), :] = s[:, b * 128:(b + 1) * 128]
        mb[...] = jnp.max(s, axis=0, keepdims=True)

    def fold(h, rows, r0, sb, mb, first):
        m = mb[...]
        if not first:
            m = jnp.maximum(ms[h], m)
            alpha = jnp.exp2((ms[h] - m) * scale)
        p = jnp.concatenate([jnp.exp2((sb[b, pl.ds(0, rows), :] - m[:, b * 128:(b + 1) * 128]) * scale) for b in range(2 * tok // 128)], axis=1)
        l = jnp.sum(p, axis=0, keepdims=True)
        o = _nn(vts[pl.ds(pl.multiple_of(h * hd, hd), hd), pl.ds(r0, rows)], p.astype(BF16))
        if not first:
            l = ls[h] * alpha + l
            o = acc[h] * alpha + o
        return m, l, o

    def keep(h, mlo):
        ms[h], ls[h], acc[h] = mlo

    def ocopy(j):
        return pltpu.make_async_remote_copy(
            src_ref=osend.at[:, pl.ds(pl.multiple_of(j * 2 * hd, 2 * hd), 2 * hd)],
            dst_ref=o_ref.at[:, pl.ds(pl.multiple_of(g0 + j * 2 * hd, 2 * hd), 2 * hd)],
            send_sem=osem.at[0, j], recv_sem=osem.at[1, j],
            device_id=mate, device_id_type=MESH)

    def attend(rows, r0, first=False, last=False):
        bufs, maxs = (sb0, sb1, sb2), (mb0, mb1, mb2)
        for d in range(AHEAD):
            scores(d, d // 2, rows, r0, bufs[d], maxs[d])

        def block(j, carry):
            even = None
            for i in range(UNROLL):
                h, k = j * UNROLL + i, i % AHEAD
                got = fold(h, rows, r0, bufs[k], maxs[k], first)
                if not last:
                    keep(h, got)
                n = jnp.minimum(h + AHEAD, heads - 1)
                scores(n, lax.div(n, 2), rows, r0, bufs[k], maxs[k])
                if last and i % 2 == 0:
                    even = got
                elif last:
                    o = jnp.concatenate([even[2] / even[1], got[2] / got[1]], axis=0).T.astype(BF16)
                    p = j * (UNROLL // 2) + i // 2
                    o_ref[:, pl.ds(pl.multiple_of(g0 + p * 2 * hd, 2 * hd), 2 * hd)] = o[:tok]
                    osend[:, pl.ds(pl.multiple_of(p * 2 * hd, 2 * hd), 2 * hd)] = o[tok:]
                    ocopy(p).start()
            return carry

        lax.fori_loop(0, heads // UNROLL, block, 0)

    for h in range(heads):
        e = ((h + 1) % 2) * hd
        qz[h, pl.ds(e, hd), :] = jnp.zeros((hd, 2 * tok), BF16)
    def project(row, r0, rows):
        project_k(row, r0, rows)
        project_v(row, r0, rows)

    loads[1].wait()
    project_q(0)
    loads[2].wait()
    loads[3].wait()
    wvt[...] = wv[...].T
    project(0, 0, tok)
    own.wait_recv()
    project_q(tok)
    project(tok, tok, tok)
    attend(2 * tok, 0, first=True)
    row, keys = 2 * tok, 0
    for s in range(6):
        arrived(s)
        rows = tok if s else tok // 2
        project(row, keys, rows)
        row, keys = row + rows, keys + rows
        if s in (1, 3, 4):
            attend(keys, 0)
            keys = 0
    from_mate[5].wait_recv()
    project(row, keys, tok // 2)
    attend(keys + tok // 2, 0, last=True)

    for j in range(heads // 2):
        ocopy(j).wait_recv()
        ocopy(j).wait_send()
    for c in (own, *from_x, *from_y, *from_mate):
        c.wait_send()


def solution(mesh):
    def body(x, w_qkv, w_o):
        tok, width = x.shape[1], x.shape[2]
        heads_all, hd = w_o.shape[0], w_o.shape[1]
        heads = heads_all // 2
        cols = heads * hd
        ncopy = 19
        o = pl.pallas_call(
            lambda *r: _kernel((tok, width, heads, hd), *r),
            out_shape=pltpu.VMEM((tok, width), BF16),
            in_specs=[pl.BlockSpec(memory_space=pltpu.HBM)] * 2,
            out_specs=pl.BlockSpec(memory_space=pltpu.VMEM),
            scratch_shapes=[
                pltpu.VMEM((8 * tok, width), BF16),
                pltpu.VMEM((width, cols), BF16),
                pltpu.VMEM((width, cols), BF16),
                pltpu.VMEM((width, cols), BF16),
                pltpu.VMEM((cols, width), BF16),
                pltpu.VMEM((2 * tok, cols), BF16),
                pltpu.VMEM((cols, 2 * tok), BF16),
                pltpu.VMEM((heads, 2 * hd, 2 * tok), BF16),
                pltpu.VMEM((heads, 1, 2 * tok), F32),
                pltpu.VMEM((heads, 1, 2 * tok), F32),
                pltpu.VMEM((heads, hd, 2 * tok), F32),
                pltpu.VMEM((tok, cols), BF16),
                pltpu.VMEM((2 * tok // 128, 2 * tok, 128), F32),
                pltpu.VMEM((2 * tok // 128, 2 * tok, 128), F32),
                pltpu.VMEM((2 * tok // 128, 2 * tok, 128), F32),
                pltpu.VMEM((1, 2 * tok), F32),
                pltpu.VMEM((1, 2 * tok), F32),
                pltpu.VMEM((1, 2 * tok), F32),
                pltpu.SemaphoreType.DMA((4,)),
                pltpu.SemaphoreType.DMA((ncopy,)),
                pltpu.SemaphoreType.DMA((ncopy,)),
                pltpu.SemaphoreType.DMA((2, heads // 2)),
            ],
            compiler_params=pltpu.CompilerParams(
                collective_id=0, has_side_effects=True, vmem_limit_bytes=48 * 1024 * 1024),
            name="dit_attention",
        )(pltpu.with_memory_space_constraint(x[0], pltpu.HBM), pltpu.with_memory_space_constraint(w_qkv, pltpu.HBM))
        y = _nn(o, w_o.reshape(heads_all * hd, width))
        return y.astype(BF16)[None]

    return jax.shard_map(
        body, mesh=mesh,
        in_specs=(P("dp", ("cx", "cy"), None), P(None, None), P(None, None, None)),
        out_specs=P("dp", ("cx", "cy"), None), check_vma=False)
```

time: 45.2 us -> 43.3 us (0.958)
  matrix products: 0 us -> 2.26 us
  Pallas kernels: 43 us -> 40.9 us
  local copies, waits for them, and re-layouts: 2.06 us -> 0.01 us
    dot_general x0 -> x1, matrix products: none -> 2.26 us  [_nn(): lax.dot_general(a, b, (((1,), (0,)), ((), ())), preferred_element_type=F32)]
    unnamed x1 -> x2, local copies, waits for them, and re-layouts: 2.06 us -> 0.01 us
    pallas_call x1, Pallas kernels: 43 us -> 40.9 us  [body(): pl.pallas_call(lambda *r: _kernel((tok, width, heads, hd), *r), out_shape...]
where the time goes in v3:
time: 43.3 us; the launch traced here: 43.2 us
  Pallas kernels  40.9 us (94%)
  matrix products  2.26 us (5%)
    pallas_call x1, Pallas kernels, body(): pl.pallas_call(lambda *r: _kernel((tok, width, heads, hd), *r), out_shape...  40.9 us
    dot_general x1, matrix products, _nn(): lax.dot_general(a, b, (((1,), (0,)), ((), ())), preferred_element_type=F32)  2.26 us

profile of v3, /device:TPU:0, one launch (start us, length us, event | category | flops | bytes accessed | tf_op | source)
XLA Modules:
  0.0 43.2 jit_solution(9937817376993030737)
XLA Ops:
  0.0 0.0 copy-start
  0.0 40.9 %dit_attention.1 = bf16[256,1536]{1,0:T(8,128)(2,1)S(1)} custom-call(bf16[256,1536]{1,0:T(8,128)(2,1)} %bitcast.6, bf16[1536,4608]{1,0:T(8,128)(2,1)} %r_1_.1), custom_call_target="tpu_custom_call" | custom-call | tf_op jit(solution)/shard_map/dit_attention/pallas_call | solution.py:203
  41.0 0.0 copy-done
  41.0 2.3 %fusion = bf16[1,256,1536]{2,1,0:T(8,128)(2,1)} fusion(bf16[256,1536]{1,0:T(8,128)(2,1)S(1)} %dit_attention.1, bf16[1536,1536]{1,0:T(8,128)(2,1)S(1)} %bitcast.7), kind=kOutput, calls=%fused_computation.1 | convolution fusion | flops 1208352768 | bytes 6291456 | tf_op jit(solution)/shard_map/dot_general | solution.py:26
Async XLA Ops:
  0.0 41.0 %copy-start = (bf16[24,64,1536]{2,1,0:T(8,128)(2,1)S(1)}, bf16[24,64,1536]{2,1,0:T(8,128)(2,1)}, u32[]{:S(2)}) copy-start(bf16[24,64,1536]{2,1,0:T(8,128)(2,1)} %param.5) | copy-start | bytes 14155780

commit v4 on v3

--- a/solution.py
+++ b/solution.py
@@ -27,7 +27,7 @@
 
 
 def _kernel(dims, x_hbm, wqkv_hbm, o_ref,
-            xs, wq, wk, wv, wvt, ks, vts, qz, ms, ls, acc, osend,
+            xs, w, ks, vts, qz, ms, ls, acc, osend,
             sb0, sb1, sb2, mb0, mb1, mb2,
             wsem, ssem, rsem, osem):
     tok, width, heads, hd = dims
@@ -46,9 +46,9 @@
     g0 = pl.multiple_of(core * cols, cols)
     loads = [
         wcopy(0, x_hbm, xs.at[pl.ds(0, tok), :]),
-        wcopy(1, wqkv_hbm.at[:, pl.ds(g0, cols)], wq),
-        wcopy(2, wqkv_hbm.at[:, pl.ds(pl.multiple_of(g0 + width, cols), cols)], wk),
-        wcopy(3, wqkv_hbm.at[:, pl.ds(pl.multiple_of(g0 + 2 * width, cols), cols)], wv),
+        wcopy(1, wqkv_hbm.at[:, pl.ds(g0, cols)], w.at[:, pl.ds(0, cols)]),
+        wcopy(2, wqkv_hbm.at[:, pl.ds(pl.multiple_of(g0 + width, cols), cols)], w.at[:, pl.ds(cols, cols)]),
+        wcopy(3, wqkv_hbm.at[:, pl.ds(pl.multiple_of(g0 + 2 * width, cols), cols)], w.at[:, pl.ds(2 * cols, cols)]),
     ]
     for ld in loads:
         ld.start()
@@ -84,21 +84,22 @@
         if s < 2:
             from_x[4 + s].start()
             from_y[4 + s].start()
-        if s > 0:
+        if 0 < s < 5:
             from_mate[s - 1].wait_recv()
 
-    def project_k(row, r0, rows):
-        ks[pl.ds(r0, rows), :] = _nn(xs[pl.ds(row, rows), :], wk[...]).astype(BF16)
-
-    def project_v(row, r0, rows):
-        vts[:, pl.ds(r0, rows)] = _nt(wvt[...], xs[pl.ds(row, rows), :]).astype(BF16)
-
-    def project_q(r0):
-        rows = xs[pl.ds(r0, tok), :]
-        qt = _nn(rows, wq[...]).T.astype(BF16)
+    def put_q(q, r0):
+        qt = q.T.astype(BF16)
         for h in range(heads):
             e = (h % 2) * hd
-            qz[h, pl.ds(e, hd), pl.ds(r0, tok)] = qt[h * hd:(h + 1) * hd, :]
+            qz[h, pl.ds(e, hd), pl.ds(r0, q.shape[0])] = qt[h * hd:(h + 1) * hd, :]
+
+    def put_kv(kv, r0):
+        rows = kv.shape[0]
+        ks[pl.ds(r0, rows), :] = kv[:, :cols].astype(BF16)
+        vts[:, pl.ds(r0, rows)] = kv[:, cols:].T.astype(BF16)
+
+    def project(row, r0, rows):
+        put_kv(_nn(xs[pl.ds(row, rows), :], w[:, pl.ds(cols, 2 * cols)]), r0)
 
     def scores(h, pair, rows, r0, sb, mb):
         kp = ks[pl.ds(r0, rows), pl.ds(pl.multiple_of(pair * 2 * hd, 2 * hd), 2 * hd)]
@@ -159,33 +160,37 @@
     for h in range(heads):
         e = ((h + 1) % 2) * hd
         qz[h, pl.ds(e, hd), :] = jnp.zeros((hd, 2 * tok), BF16)
-    def project(row, r0, rows):
-        project_k(row, r0, rows)
-        project_v(row, r0, rows)
-
     loads[1].wait()
-    project_q(0)
+    put_q(_nn(xs[pl.ds(0, tok), :], w[:, pl.ds(0, cols)]), 0)
+    own.wait_recv()
     loads[2].wait()
     loads[3].wait()
-    wvt[...] = wv[...].T
     project(0, 0, tok)
-    own.wait_recv()
-    project_q(tok)
-    project(tok, tok, tok)
+    qkv = _nn(xs[pl.ds(tok, tok), :], w[...])
+    put_q(qkv[:, :cols], tok)
+    put_kv(qkv[:, cols:], tok)
     attend(2 * tok, 0, first=True)
+
     row, keys = 2 * tok, 0
+
+    def take(rows):
+        nonlocal row, keys
+        project(row, keys, rows)
+        row, keys = row + rows, keys + rows
+
+    half = tok // 2
     for s in range(6):
         arrived(s)
-        rows = tok if s else tok // 2
-        project(row, keys, rows)
-        row, keys = row + rows, keys + rows
-        if s in (1, 3, 4):
-            attend(keys, 0)
+        take(tok if s in (1, 2, 3, 4) else half)
+        if s == 4:
+            from_mate[4].wait_recv()
+            take(half)
+        if s == 5:
+            from_mate[5].wait_recv()
+            take(half)
+        if s > 0:
+            attend(keys, 0, last=s == 5)
             keys = 0
-    from_mate[5].wait_recv()
-    project(row, keys, tok // 2)
-    attend(keys + tok // 2, 0, last=True)
-
     for j in range(heads // 2):
         ocopy(j).wait_recv()
         ocopy(j).wait_send()
@@ -207,10 +212,7 @@
             out_specs=pl.BlockSpec(memory_space=pltpu.VMEM),
             scratch_shapes=[
                 pltpu.VMEM((8 * tok, width), BF16),
-                pltpu.VMEM((width, cols), BF16),
-                pltpu.VMEM((width, cols), BF16),
-                pltpu.VMEM((width, cols), BF16),
-                pltpu.VMEM((cols, width), BF16),
+                pltpu.VMEM((width, 3 * cols), BF16),
                 pltpu.VMEM((2 * tok, cols), BF16),
                 pltpu.VMEM((cols, 2 * tok), BF16),
                 pltpu.VMEM((heads, 2 * hd, 2 * tok), BF16),

time: 43.3 us -> 41.7 us (0.963)
  Pallas kernels: 40.9 us -> 39.3 us
    pallas_call x1, Pallas kernels: 40.9 us -> 39.3 us  [body(): pl.pallas_call(lambda *r: _kernel((tok, width, heads, hd), *r), out_shape...]
where the time goes in v4:
time: 41.7 us; the launch traced here: 41.6 us
  Pallas kernels  39.3 us (94%)
  matrix products  2.27 us (5%)
    pallas_call x1, Pallas kernels, body(): pl.pallas_call(lambda *r: _kernel((tok, width, heads, hd), *r), out_shape...  39.3 us
    dot_general x1, matrix products, _nn(): lax.dot_general(a, b, (((1,), (0,)), ((), ())), preferred_element_type=F32)  2.27 us

profile of v4, /device:TPU:0, one launch (start us, length us, event | category | flops | bytes accessed | tf_op | source)
XLA Modules:
  0.0 41.6 jit_solution(15409168819932911560)
XLA Ops:
  0.0 0.0 copy-start
  0.0 39.3 %dit_attention.1 = bf16[256,1536]{1,0:T(8,128)(2,1)S(1)} custom-call(bf16[256,1536]{1,0:T(8,128)(2,1)} %bitcast.6, bf16[1536,4608]{1,0:T(8,128)(2,1)} %r_1_.1), custom_call_target="tpu_custom_call" | custom-call | tf_op jit(solution)/shard_map/dit_attention/pallas_call | solution.py:208
  39.3 0.0 copy-done
  39.3 2.3 %fusion = bf16[1,256,1536]{2,1,0:T(8,128)(2,1)} fusion(bf16[256,1536]{1,0:T(8,128)(2,1)S(1)} %dit_attention.1, bf16[1536,1536]{1,0:T(8,128)(2,1)S(1)} %bitcast.7), kind=kOutput, calls=%fused_computation.1 | convolution fusion | flops 1208352768 | bytes 6291456 | tf_op jit(solution)/shard_map/dot_general | solution.py:26
Async XLA Ops:
  0.0 39.3 %copy-start = (bf16[24,64,1536]{2,1,0:T(8,128)(2,1)S(1)}, bf16[24,64,1536]{2,1,0:T(8,128)(2,1)}, u32[]{:S(2)}) copy-start(bf16[24,64,1536]{2,1,0:T(8,128)(2,1)} %param.5) | copy-start | bytes 14155780

commit v5 on v4

--- a/solution.py
+++ b/solution.py
@@ -11,7 +11,7 @@
 BF16 = jnp.bfloat16
 F32 = jnp.float32
 UNROLL = 6
-AHEAD = 3
+AHEAD = 2
 
 
 def _nt(a, b):
@@ -26,8 +26,8 @@
     return lax.dot_general(a, b, (((1,), (0,)), ((), ())), preferred_element_type=F32)
 
 
-def _kernel(dims, x_hbm, wqkv_hbm, o_ref,
-            xs, w, ks, vts, qz, ms, ls, acc, osend,
+def _kernel(dims, x_hbm, wqkv_hbm, wo_hbm, y_ref,
+            xs, w, wo, part_ref, o_ref, wo_ref, ks, vts, qz, ms, ls, acc, omine, osend,
             sb0, sb1, sb2, mb0, mb1, mb2,
             wsem, ssem, rsem, osem):
     tok, width, heads, hd = dims
@@ -36,6 +36,7 @@
 
     dp, cx, cy = lax.axis_index("dp"), lax.axis_index("cx"), lax.axis_index("cy")
     core = lax.rem(cy, 2)
+    one = 1 + lax.div(core, 2)
     mate = (dp, cx, cy + 1 - 2 * core)
     xn = (dp, cx, lax.rem(cy + 2, 4))
     yn = (dp, 1 - cx, cy)
@@ -52,6 +53,8 @@
     ]
     for ld in loads:
         ld.start()
+    g1 = pl.multiple_of((1 - core) * cols, cols)
+    wo_loads = [wcopy(4, wo_hbm.at[pl.ds(g0, cols), :], wo), wcopy(5, wo_hbm.at[pl.ds(g1, cols), :], wo_ref)]
 
     barrier = pltpu.get_barrier_semaphore()
     for other in (mate, xn, yn):
@@ -84,7 +87,7 @@
         if s < 2:
             from_x[4 + s].start()
             from_y[4 + s].start()
-        if 0 < s < 5:
+        if s > 0:
             from_mate[s - 1].wait_recv()
 
     def put_q(q, r0):
@@ -127,7 +130,7 @@
     def ocopy(j):
         return pltpu.make_async_remote_copy(
             src_ref=osend.at[:, pl.ds(pl.multiple_of(j * 2 * hd, 2 * hd), 2 * hd)],
-            dst_ref=o_ref.at[:, pl.ds(pl.multiple_of(g0 + j * 2 * hd, 2 * hd), 2 * hd)],
+            dst_ref=o_ref.at[:, pl.ds(pl.multiple_of(j * 2 * hd, 2 * hd), 2 * hd)],
             send_sem=osem.at[0, j], recv_sem=osem.at[1, j],
             device_id=mate, device_id_type=MESH)
 
@@ -136,26 +139,30 @@
         for d in range(AHEAD):
             scores(d, d // 2, rows, r0, bufs[d], maxs[d])
 
-        def block(j, carry):
+        def block(j):
             even = None
             for i in range(UNROLL):
-                h, k = j * UNROLL + i, i % AHEAD
+                h = j * UNROLL + i
+                k, n = h % 3, (h + AHEAD) % 3
+                if h + AHEAD < heads:
+                    scores(h + AHEAD, (h + AHEAD) // 2, rows, r0, bufs[n], maxs[n])
                 got = fold(h, rows, r0, bufs[k], maxs[k], first)
                 if not last:
                     keep(h, got)
-                n = jnp.minimum(h + AHEAD, heads - 1)
-                scores(n, lax.div(n, 2), rows, r0, bufs[k], maxs[k])
                 if last and i % 2 == 0:
                     even = got
                 elif last:
-                    o = jnp.concatenate([even[2] / even[1], got[2] / got[1]], axis=0).T.astype(BF16)
-                    p = j * (UNROLL // 2) + i // 2
-                    o_ref[:, pl.ds(pl.multiple_of(g0 + p * 2 * hd, 2 * hd), 2 * hd)] = o[:tok]
-                    osend[:, pl.ds(pl.multiple_of(p * 2 * hd, 2 * hd), 2 * hd)] = o[tok:]
+                    o = jnp.concatenate([even[2] * (1.0 / even[1]), got[2] * (1.0 / got[1])], axis=0).T.astype(BF16)
+                    p = h // 2
+                    omine[:, pl.ds(p * 2 * hd, 2 * hd)] = o[:tok]
+                    osend[:, pl.ds(p * 2 * hd, 2 * hd)] = o[tok:]
                     ocopy(p).start()
-            return carry
-
-        lax.fori_loop(0, heads // UNROLL, block, 0)
+
+        for j in range(heads // UNROLL):
+            def body(_, carry, j=j):
+                block(j)
+                return carry
+            lax.fori_loop(0, one, body, 0)
 
     for h in range(heads):
         e = ((h + 1) % 2) * hd
@@ -171,6 +178,8 @@
     put_kv(qkv[:, cols:], tok)
     attend(2 * tok, 0, first=True)
 
+    for ld in wo_loads:
+        ld.start()
     row, keys = 2 * tok, 0
 
     def take(rows):
@@ -178,24 +187,41 @@
         project(row, keys, rows)
         row, keys = row + rows, keys + rows
 
-    half = tok // 2
     for s in range(6):
         arrived(s)
-        take(tok if s in (1, 2, 3, 4) else half)
-        if s == 4:
-            from_mate[4].wait_recv()
-            take(half)
-        if s == 5:
-            from_mate[5].wait_recv()
-            take(half)
-        if s > 0:
-            attend(keys, 0, last=s == 5)
+        take(tok if s else tok // 2)
+        if 0 < s < 5:
+            attend(keys, 0)
             keys = 0
+    for c in (own, *from_x, *from_y, *from_mate[:5]):
+        c.wait_send()
+    from_mate[5].wait_recv()
+    take(tok // 2)
+    attend(keys, 0, last=True)
+    for ld in wo_loads:
+        ld.wait()
+    early, late = pl.ds(0, cols // 2), pl.ds(cols // 2, cols // 2)
+    for j in range(heads // 4):
+        ocopy(j).wait_recv()
+    part_ref[...] = _nn(omine[...], wo[...]) + _nn(o_ref[:, early], wo_ref[early, :])
+    for j in range(heads // 4, heads // 2):
+        ocopy(j).wait_recv()
+    y_ref[...] = (part_ref[...] + _nn(o_ref[:, late], wo_ref[late, :])).astype(BF16)
     for j in range(heads // 2):
-        ocopy(j).wait_recv()
         ocopy(j).wait_send()
-    for c in (own, *from_x, *from_y, *from_mate):
-        c.wait_send()
+    from_mate[5].wait_send()
+
+
+def _finish(part_ref, o_ref, wo_ref, y_hbm, buf, sem):
+    n, _, block = buf.shape
+    outs = []
+    for i in range(n):
+        at = pl.ds(i * block, block)
+        buf[i] = (part_ref[:, at] + _nn(o_ref[...], wo_ref[:, at])).astype(BF16)
+        outs.append(pltpu.make_async_copy(buf.at[i], y_hbm.at[:, at], sem.at[i]))
+        outs[-1].start()
+    for out in outs:
+        out.wait()
 
 
 def solution(mesh):
@@ -205,14 +231,19 @@
         heads = heads_all // 2
         cols = heads * hd
         ncopy = 19
-        o = pl.pallas_call(
+        hbm = lambda a: pltpu.with_memory_space_constraint(a, pltpu.HBM)
+        y = pl.pallas_call(
             lambda *r: _kernel((tok, width, heads, hd), *r),
             out_shape=pltpu.VMEM((tok, width), BF16),
-            in_specs=[pl.BlockSpec(memory_space=pltpu.HBM)] * 2,
+            in_specs=[pl.BlockSpec(memory_space=pltpu.HBM)] * 3,
             out_specs=pl.BlockSpec(memory_space=pltpu.VMEM),
             scratch_shapes=[
                 pltpu.VMEM((8 * tok, width), BF16),
                 pltpu.VMEM((width, 3 * cols), BF16),
+                pltpu.VMEM((cols, width), BF16),
+                pltpu.VMEM((tok, width), F32),
+                pltpu.VMEM((tok, cols), BF16),
+                pltpu.VMEM((cols, width), BF16),
                 pltpu.VMEM((2 * tok, cols), BF16),
                 pltpu.VMEM((cols, 2 * tok), BF16),
                 pltpu.VMEM((heads, 2 * hd, 2 * tok), BF16),
@@ -220,13 +251,14 @@
                 pltpu.VMEM((heads, 1, 2 * tok), F32),
                 pltpu.VMEM((heads, hd, 2 * tok), F32),
                 pltpu.VMEM((tok, cols), BF16),
+                pltpu.VMEM((tok, cols), BF16),
                 pltpu.VMEM((2 * tok // 128, 2 * tok, 128), F32),
                 pltpu.VMEM((2 * tok // 128, 2 * tok, 128), F32),
                 pltpu.VMEM((2 * tok // 128, 2 * tok, 128), F32),
                 pltpu.VMEM((1, 2 * tok), F32),
                 pltpu.VMEM((1, 2 * tok), F32),
                 pltpu.VMEM((1, 2 * tok), F32),
-                pltpu.SemaphoreType.DMA((4,)),
+                pltpu.SemaphoreType.DMA((6,)),
                 pltpu.SemaphoreType.DMA((ncopy,)),
                 pltpu.SemaphoreType.DMA((ncopy,)),
                 pltpu.SemaphoreType.DMA((2, heads // 2)),
@@ -234,9 +266,8 @@
             compiler_params=pltpu.CompilerParams(
                 collective_id=0, has_side_effects=True, vmem_limit_bytes=48 * 1024 * 1024),
             name="dit_attention",
-        )(pltpu.with_memory_space_constraint(x[0], pltpu.HBM), pltpu.with_memory_space_constraint(w_qkv, pltpu.HBM))
-        y = _nn(o, w_o.reshape(heads_all * hd, width))
-        return y.astype(BF16)[None]
+        )(hbm(x[0]), hbm(w_qkv), hbm(w_o.reshape(heads_all * hd, width)))
+        return y[None]
 
     return jax.shard_map(
         body, mesh=mesh,

time: 41.7 us -> 39.7 us (0.952)
  matrix products: 2.27 us -> 0 us
  local copies, waits for them, and re-layouts: 0.01 us -> 0.88 us
  Pallas kernels: 39.3 us -> 38.7 us
    dot_general x1 -> x0, matrix products: 2.27 us -> none  [_nn(): lax.dot_general(a, b, (((1,), (0,)), ((), ())), preferred_element_type=F32)]
    unnamed x2 -> x1, local copies, waits for them, and re-layouts: 0.01 us -> 0.88 us
    pallas_call x1, Pallas kernels: 39.3 us -> 38.7 us  [body(): pl.pallas_call(lambda *r: _kernel((tok, width, heads, hd), *r), out_shape...]
where the time goes in v5:
time: 39.7 us; the launch traced here: 39.6 us
  Pallas kernels  38.7 us (97%)
  local copies, waits for them, and re-layouts  0.88 us (2%)
    pallas_call x1, Pallas kernels, body(): pl.pallas_call(lambda *r: _kernel((tok, width, heads, hd), *r), out_shape...  38.7 us
    unnamed x1, local copies, waits for them, and re-layouts  0.88 us

profile of v5, /device:TPU:0, one launch (start us, length us, event | category | flops | bytes accessed | tf_op | source)
XLA Modules:
  0.0 39.6 jit_solution(670106628650905659)
XLA Ops:
  0.0 38.7 %dit_attention.1 = bf16[256,1536]{1,0:T(8,128)(2,1)S(1)} custom-call(bf16[256,1536]{1,0:T(8,128)(2,1)} %bitcast.5, bf16[1536,4608]{1,0:T(8,128)(2,1)} %r_1_.1, bf16[1536,1536]{1,0:T(8,128)(2,1)} %bitcast.4), custom_call_target="tpu_custom_call" | custom-call | tf_op jit(solution)/shard_map/dit_attention/pallas_call | solution.py:235
  38.7 0.9 %copy.5 = bf16[1,256,1536]{2,1,0:T(8,128)(2,1)} copy(bf16[1,256,1536]{2,1,0:T(8,128)(2,1)S(1)} %bitcast.3) | data formatting | bytes 1572864
